TPU v7x, 32 devices: a whole 2x2x4 slice. The times are simulated.
32 devices in a mesh: prefix: 4 (over z), resp: 8 (over y, x, core).
Axes of the slice: x: 2, y: 2, z: 4, core: 2. Of those that a mesh axis runs over, the one named last changes fastest.
Arguments:
- prompt_kv: bfloat16 [2, 128, 512], P(None, 'prefix'), may hold values from -6 to 6
- response_queries: bfloat16 [64, 128, 1792], P(('prefix', 'resp')), may hold values from -300 to 300
- resp_kv: bfloat16 [64, 128, 512], P(('prefix', 'resp')), may hold values from -6 to 6
- readout: bfloat16 [64, 128, 1792], P(('prefix', 'resp')), may hold values from -3 to 3
- slot_response: int32 [64], P(('prefix', 'resp')), may hold values from 0 to 63, each once
- lengths: int32 [64], replicated, may hold values from 32 to 128
- pair_prompt: int32 [32], replicated, may hold values from 0 to 1
- ref_margin: float32 [32], replicated, may hold values from -60 to 60
Outputs:
- margins: float32 [32], replicated
- grad_q: bfloat16 [64, 128, 1792], P(('prefix', 'resp'))
- grad_resp_kv: bfloat16 [64, 128, 512], P(('prefix', 'resp'))
- grad_prompt_kv: bfloat16 [2, 128, 512], P(None, 'prefix')
Inputs may be any that keep to these rules, and one draw needn't show every extreme that they name: `slot_response`: each response appears in exactly one slot; response 2 k is the chosen and 2 k + 1 the rejected response of pair k.
All inputs are finite; a program needn't handle non-finite values.
Results may differ from a plain program's by a relative error of at most 0.015.
Values may be sent and summed in bfloat16 or wider, within the bound.
A program may use at most 64 MiB of HBM per device.

v0:
```python
import jax
import jax.numpy as jnp
from jax import lax
from jax.sharding import PartitionSpec as P

QUERY_HEADS = 14
KEY_VALUE_HEADS = 2
HEAD_SIZE = 128
margin_beta = 0.1
loss_scale = 256.0


def unpack(packed_rows):
    row_block = packed_rows.shape[0]
    head_width = packed_rows.shape[1] // 2
    key_rows = packed_rows[:, :head_width].reshape(row_block, KEY_VALUE_HEADS, HEAD_SIZE)
    value_rows = packed_rows[:, head_width:].reshape(row_block, KEY_VALUE_HEADS, HEAD_SIZE)
    return (key_rows, value_rows)


def forward_pieces(query_rows, prompt_packed, own_packed, causal):
    prompt_keys, prompt_values = unpack(prompt_packed)
    own_keys, own_values = unpack(own_packed)
    scale_factor = HEAD_SIZE ** (-0.5)
    prompt_scores = (
        jnp.einsum("tgjd,kgd->gjtk", query_rows, prompt_keys, preferred_element_type=jnp.float32)
        * scale_factor
    )
    own_scores = (
        jnp.einsum("tgjd,kgd->gjtk", query_rows, own_keys, preferred_element_type=jnp.float32)
        * scale_factor
    )
    own_scores = jnp.where(causal, own_scores, -jnp.inf)
    row_max = jnp.maximum(
        jnp.max(prompt_scores, -1, keepdims=True), jnp.max(own_scores, -1, keepdims=True)
    )
    prompt_exp = jnp.exp(prompt_scores - row_max)
    own_exp = jnp.exp(own_scores - row_max)
    total = jnp.sum(prompt_exp, -1, keepdims=True) + jnp.sum(own_exp, -1, keepdims=True)
    prefix_probabilities = (prompt_exp / total).astype(jnp.bfloat16)
    self_probabilities = (own_exp / total).astype(jnp.bfloat16)
    attended = jnp.einsum(
        "gjtk,kgd->tgjd", prefix_probabilities, prompt_values, preferred_element_type=jnp.float32
    )
    attended = attended + jnp.einsum(
        "gjtk,kgd->tgjd", self_probabilities, own_values, preferred_element_type=jnp.float32
    )
    return (
        prompt_keys,
        prompt_values,
        own_keys,
        own_values,
        prefix_probabilities,
        self_probabilities,
        attended,
    )


def on_device(
    prompt_kv, response_queries, resp_kv, readout, slot_response, lengths, pair_prompt, ref_margin
):
    prompts = prompt_kv.shape[0]
    slots, slot_capacity, query_width = response_queries.shape
    query_groups = QUERY_HEADS // KEY_VALUE_HEADS
    pairs = ref_margin.shape[0]
    scale_factor = HEAD_SIZE ** (-0.5)
    full_kv = lax.all_gather(prompt_kv, "prefix", axis=1, tiled=True)
    prefix_length = full_kv.shape[1]
    positions = jnp.arange(slot_capacity)
    causal = positions[None, :] <= positions[:, None]
    pair_ids = jnp.arange(pairs)
    prompt_ids = jnp.arange(prompts)
    contrib = jnp.zeros((pairs,), jnp.float32)
    saved = []
    for position_index in range(slots):
        response = slot_response[position_index]
        pair_index = response // 2
        sign = 1.0 - 2.0 * (response % 2).astype(jnp.float32)
        valid = (positions < lengths[response]).astype(jnp.float32)
        prompt_index = pair_prompt[pair_index]
        prompt_packed = lax.dynamic_index_in_dim(full_kv, prompt_index, 0, keepdims=False)
        query_rows = response_queries[position_index].reshape(
            slot_capacity, KEY_VALUE_HEADS, query_groups, HEAD_SIZE
        )
        output_rows = readout[position_index].reshape(
            slot_capacity, KEY_VALUE_HEADS, query_groups, HEAD_SIZE
        )
        pieces = forward_pieces(query_rows, prompt_packed, resp_kv[position_index], causal)
        token_logp = jnp.sum(pieces[-1] * output_rows.astype(jnp.float32), axis=(1, 2, 3)) * valid
        contrib = contrib + jnp.where(pair_ids == pair_index, sign * jnp.sum(token_logp), 0.0)
        saved.append((pair_index, sign, valid, prompt_index, query_rows, output_rows, pieces))
    pair_sums = lax.psum(contrib, ("prefix", "resp"))
    margins = margin_beta * (pair_sums - ref_margin)
    weights = -loss_scale * margin_beta * jax.nn.sigmoid(-margins)
    partial_value = jnp.zeros((prompts, prefix_length, full_kv.shape[2]), jnp.float32)
    grad_rows = []
    grad_own = []
    for pair_index, sign, valid, prompt_index, query_rows, output_rows, pieces in saved:
        (
            prompt_keys,
            prompt_values,
            own_keys,
            own_values,
            prefix_probabilities,
            self_probabilities,
            attended,
        ) = pieces
        coefficient = weights[pair_index] * sign
        output_gradient = (
            coefficient * output_rows.astype(jnp.float32) * valid[:, None, None, None]
        ).astype(jnp.bfloat16)
        prompt_dprobs = jnp.einsum(
            "tgjd,kgd->gjtk", output_gradient, prompt_values, preferred_element_type=jnp.float32
        )
        own_dprobs = jnp.einsum(
            "tgjd,kgd->gjtk", output_gradient, own_values, preferred_element_type=jnp.float32
        )
        delta = jnp.transpose(
            jnp.sum(output_gradient.astype(jnp.float32) * attended, -1), (1, 2, 0)
        )[..., None]
        prefix_score_gradient = (
            prefix_probabilities.astype(jnp.float32) * (prompt_dprobs - delta) * scale_factor
        ).astype(jnp.bfloat16)
        self_score_gradient = (
            self_probabilities.astype(jnp.float32) * (own_dprobs - delta) * scale_factor
        ).astype(jnp.bfloat16)
        grad_queries = jnp.einsum(
            "gjtk,kgd->tgjd", prefix_score_gradient, prompt_keys, preferred_element_type=jnp.float32
        )
        grad_queries = grad_queries + jnp.einsum(
            "gjtk,kgd->tgjd", self_score_gradient, own_keys, preferred_element_type=jnp.float32
        )
        prompt_grad = jnp.concatenate(
            [
                jnp.einsum(
                    "hybi,bhyu->ihu",
                    prefix_score_gradient,
                    query_rows,
                    preferred_element_type=jnp.float32,
                ).reshape(prefix_length, KEY_VALUE_HEADS * HEAD_SIZE),
                jnp.einsum(
                    "hybi,bhyu->ihu",
                    prefix_probabilities,
                    output_gradient,
                    preferred_element_type=jnp.float32,
                ).reshape(prefix_length, KEY_VALUE_HEADS * HEAD_SIZE),
            ],
            axis=-1,
        )
        own_grad = jnp.concatenate(
            [
                jnp.einsum(
                    "hybi,bhyu->ihu",
                    self_score_gradient,
                    query_rows,
                    preferred_element_type=jnp.float32,
                ).reshape(slot_capacity, KEY_VALUE_HEADS * HEAD_SIZE),
                jnp.einsum(
                    "hybi,bhyu->ihu",
                    self_probabilities,
                    output_gradient,
                    preferred_element_type=jnp.float32,
                ).reshape(slot_capacity, KEY_VALUE_HEADS * HEAD_SIZE),
            ],
            axis=-1,
        )
        selector = (prompt_ids == prompt_index)[:, None, None]
        partial_value = partial_value + jnp.where(selector, prompt_grad[None], 0.0)
        grad_rows.append(grad_queries.reshape(slot_capacity, query_width).astype(jnp.bfloat16))
        grad_own.append(own_grad.astype(jnp.bfloat16))
    owned = lax.psum_scatter(partial_value, "prefix", scatter_dimension=1, tiled=True)
    grad_prompt = lax.psum(owned, "resp").astype(jnp.bfloat16)
    return (margins, jnp.stack(grad_rows), jnp.stack(grad_own), grad_prompt)


def solution(mesh):
    in_specs = (
        P(None, "prefix", None),
        P(("prefix", "resp"), None, None),
        P(("prefix", "resp"), None, None),
        P(("prefix", "resp"), None, None),
        P(("prefix", "resp")),
        P(),
        P(),
        P(),
    )
    out_specs = (
        P(),
        P(("prefix", "resp"), None, None),
        P(("prefix", "resp"), None, None),
        P(None, "prefix", None),
    )
    return jax.shard_map(
        on_device, mesh=mesh, in_specs=in_specs, out_specs=out_specs, check_vma=False
    )
```

profile of v0, /device:TPU:0, one launch (start us, length us, event | category | flops | bytes accessed | tf_op | source)
XLA Modules:
  0.0 167.4 jit_solution(1739317058117866416)
XLA Ops:
  7.2 1.3 fusion.48
  15.1 0.6 fusion.47
  18.3 1.9 %iota_compare_fusion.1 = (pred[2]{0:T(512)(128)(4,1)}, pred[2]{0:T(512)(128)(4,1)}) fusion(s32[]{:T(128)} %bitcast.23, s32[]{:T(128)} %bitcast.2), kind=kLoop, calls=%fused_computation.89 | loop fusion | flops 4 | bytes 12 | tf_op jit(solution)/shard_map/eq | solution.py:167
  21.5 0.6 copy-done.24
  22.2 0.6 fusion.46
  22.8 1.2 compare_convert_fusion.1
  24.0 15.6 %all_gather.3 = bf16[2,128,512]{2,1,0:T(8,128)(2,1)S(1)} all-gather(bf16[2,32,512]{2,1,0:T(8,128)(2,1)S(1)} %copy-done.20), channel_id=1, replica_groups=mesh['prefix'=4,'resp'=8] {'prefix'}, dimensions={1}, use_global_device_ids=true | all-gather | bytes 327680 | tf_op jit(solution)/shard_map/all_gather | solution.py:67
  42.2 0.6 fusion.44
  44.5 1.1 divide_convert_fusion.1
  47.0 0.8 copy-done.12
  47.8 1.5 slice_convert_fusion.1
  49.3 1.5 copy.68
  51.1 1.2 multiply_reduce_fusion.3
  52.3 1.2 fusion.36
  53.5 1.5 copy.79
  55.0 2.0 %convolution_bitcast_fusion.2 = f32[128,2,7,128]{0,3,2,1:T(8,128)} fusion(bf16[128,2,128,1]{0,2,3,1:T(8,128)(2,1)} %bitcast.294, bf16[2,7,128,128]{2,3,1,0:T(8,128)(2,1)S(1)} %get-tuple-element.33), kind=kOutput, calls=%fused_computation.2 | convolution fusion | flops 58720256 | bytes 1441792 | tf_op jit(solution)/shard_map/gjtk,kgd->tgjd/dot_general | solution.py:45
  57.6 2.6 %multiply_reduce_fusion.2 = (f32[128]{0:T(128)S(1)}, f32[128,2,7,128]{0,3,2,1:T(8,128)}) fusion(f32[128,2,7,128]{0,3,2,1:T(8,128)S(1)} %bitcast.278, f32[128,2,7,128]{0,3,2,1:T(8,128)} %convolution_bitcast_fusion.2, bf16[128,2,128,1]{0,2,3,1:T(8,128)(2,1)S(1)} %bitcast.284, bf16[2,7,128,128]{2,3,1,0:T(8,128)(2,1)} %get-tuple-element.32), kind=kOutput, calls=%fused_computation.57 | convolution fusion | flops 59408256 | bytes 3277312 | tf_op jit(solution)/shard_map/gjtk,kgd->tgjd/dot_general | solution.py:42
  60.2 1.2 fusion.37
  62.1 0.6 compare_convert_fusion
  62.7 40.7 %psum.14 = f32[32]{0:T(128)S(1)} all-reduce(f32[32]{0:T(128)S(1)} %fusion.38), channel_id=1, replica_groups=mesh['prefix'=4,'resp'=8] {'prefix','resp'}, use_global_device_ids=true, to_apply=%region_12.13 | all-reduce | flops 32 | bytes 256 | tf_op jit(solution)/shard_map/psum | solution.py:92
  105.6 0.6 copy-done.26
  106.2 1.4 multiply_reduce_fusion.1
  109.3 1.4 multiply_reduce_fusion
  113.0 0.9 select_add_fusion
  114.0 1.0 copy-done.3
  115.0 0.9 fusion.29
  116.3 0.6 copy-done.1
  121.6 0.7 copy-done.8
  122.8 0.7 maximum_maximum_fusion
  123.5 1.0 pad_maximum_fusion
  124.6 11.3 %reduce-scatter.2.cloned.1.call-done = f32[2,32,512]{2,1,0:T(8,128)} async-done(((f32[2,128,512]{2,1,0:T(8,128)}), f32[2,32,512]{2,1,0:T(8,128)}) %reduce-scatter.2.cloned.1.call-update) | async-done | bytes 131088 | tf_op jit(solution)/shard_map/reduce_scatter | solution.py:171
  135.9 24.7 %all-reduce.1 = bf16[2,32,512]{2,1,0:T(8,128)(2,1)} all-reduce(f32[2,32,512]{2,1,0:T(8,128)} %reduce-scatter.2.cloned.1.call-done), channel_id=1, replica_groups=mesh['prefix'=4,'resp'=8] {'resp'}, use_global_device_ids=true, to_apply=%region_16.17 | all-reduce | flops 32768 | bytes 196608 | tf_op jit(solution)/shard_map/psum | solution.py:172
  (104 shorter events, 14.9 us)
Async XLA Ops:
  7.2 128.7 %reduce-scatter.2.cloned.1.call-start = ((), (), s32[]{:S(2)}) async-start(), calls=%async_computation.1 | async-start | bytes 655360 | tf_op jit(solution)/shard_map/reduce_scatter | solution.py:171
  11.8 3.3 %copy-start.23 = (s32[32]{0:T(128)S(1)}, s32[32]{0:T(128)}, u32[]{:S(2)}) copy-start(s32[32]{0:T(128)} %param.14) | copy-start | bytes 388
  11.8 12.2 %copy-start.20 = (bf16[2,32,512]{2,1,0:T(8,128)(2,1)S(1)}, bf16[2,32,512]{2,1,0:T(8,128)(2,1)}, u32[]{:S(2)}) copy-start(bf16[2,32,512]{2,1,0:T(8,128)(2,1)} %param.8) | copy-start | bytes 196612
  21.5 0.7 copy-start.24
  41.0 1.0 copy-start.18
  41.2 4.7 %copy-start.14 = (bf16[128,256]{0,1:T(8,128)(2,1)}, bf16[128,256]{0,1:T(8,128)(2,1)S(1)}, u32[]{:S(2)}) copy-start(bf16[128,256]{0,1:T(8,128)(2,1)S(1)} %copy.59) | copy-start | bytes 196612
  41.2 1.6 copy-start.11
  41.4 2.1 %copy-start.16 = (bf16[128,256]{0,1:T(8,128)(2,1)}, bf16[128,256]{0,1:T(8,128)(2,1)S(1)}, u32[]{:S(2)}) copy-start(bf16[128,256]{0,1:T(8,128)(2,1)S(1)} %copy.70) | copy-start | bytes 196612
  45.6 9.4 %copy-start = (bf16[2,7,128,128]{2,3,1,0:T(8,128)(2,1)}, bf16[2,7,128,128]{2,3,1,0:T(8,128)(2,1)S(1)}, u32[]{:S(2)}) copy-start(bf16[2,7,128,128]{2,3,1,0:T(8,128)(2,1)S(1)} %get-tuple-element.33) | copy-start | bytes 1376260
  46.7 1.2 copy-start.12
  47.8 3.0 %copy-start.2 = (bf16[2,7,128,128]{2,3,1,0:T(8,128)(2,1)}, bf16[2,7,128,128]{2,3,1,0:T(8,128)(2,1)S(1)}, u32[]{:S(2)}) copy-start(bf16[2,7,128,128]{2,3,1,0:T(8,128)(2,1)S(1)} %get-tuple-element.31) | copy-start | bytes 1376260
  47.8 3.2 %copy-start.5 = (bf16[2,7,128,128]{2,3,1,0:T(8,128)(2,1)}, bf16[2,7,128,128]{2,3,1,0:T(8,128)(2,1)S(1)}, u32[]{:S(2)}) copy-start(bf16[2,7,128,128]{2,3,1,0:T(8,128)(2,1)S(1)} %get-tuple-element.30) | copy-start | bytes 1376260
  62.7 40.7 %copy-start.25 = (f32[32]{0:T(128)S(1)}, f32[32]{0:T(128)}, u32[]{:S(2)}) copy-start(f32[32]{0:T(128)} %param.15) | copy-start | bytes 388
  105.6 0.6 copy-start.26
  106.2 1.4 copy-start.6
  108.3 0.8 copy-start.7
  109.3 1.4 copy-start.4
  111.4 0.8 copy-start.9
  112.3 0.6 copy-start.21
  112.3 0.7 copy-start.22
  113.9 1.0 copy-start.3
  115.9 1.0 copy-start.1
  116.9 0.8 copy-start.13
  118.4 0.8 copy-start.19
  119.4 1.0 copy-start.10
  119.9 0.9 copy-start.17
  121.3 1.0 copy-start.8
  121.3 1.0 copy-start.15
Sparse Core Ops, SparseCore 0:
  114.1 21.7 reduce-scatter.1
where the time goes:
time: 169 us; the launch traced here: 167 us
  blocking collectives  81 us (48%)
  between operations  28.7 us (17%)
  local copies, waits for them, and re-layouts  17.5 us (10%)
  other arithmetic  15.8 us (9%)
  matrix products  13 us (8%)
  waiting for transfers between devices  11.4 us (7%)
    psum x1, blocking collectives, on_device(): pair_sums = lax.psum(contrib, ('prefix', 'resp'))  40.7 us
    psum x1, blocking collectives, on_device(): grad_prompt = lax.psum(owned, 'resp').astype(jnp.bfloat16)  24.7 us
    all_gather x1, blocking collectives, on_device(): full_kv = lax.all_gather(prompt_kv, 'prefix', axis=1, tiled=True)  15.6 us
    reduce_scatter x1, waiting for transfers between devices, on_device(): lax.psum_scatter(partial_value, 'prefix', scatter_dimension=1, tiled=True)  11.3 us
    unnamed x58, local copies, waits for them, and re-layouts  9.16 us
    dot_general x2, matrix products, forward_pieces(): jnp.einsum('gjtk,kgd->tgjd', prefix_probabilities, prompt_values, preferr...  3.82 us
  transfers between devices with their start and end apart: 1, of which 1 were waited for; matrix products, arithmetic and copies ran while one was open for 4% of the time, Pallas kernels for 0%

commit v1 on v0

--- a/solution.py
+++ b/solution.py
@@ -89,7 +89,8 @@
         token_logp = jnp.sum(pieces[-1] * output_rows.astype(jnp.float32), axis=(1, 2, 3)) * valid
         contrib = contrib + jnp.where(pair_ids == pair_index, sign * jnp.sum(token_logp), 0.0)
         saved.append((pair_index, sign, valid, prompt_index, query_rows, output_rows, pieces))
-    pair_sums = lax.psum(contrib, ("prefix", "resp"))
+    inner = lax.psum(contrib, "resp")
+    pair_sums = lax.psum(inner, "prefix")
     margins = margin_beta * (pair_sums - ref_margin)
     weights = -loss_scale * margin_beta * jax.nn.sigmoid(-margins)
     partial_value = jnp.zeros((prompts, prefix_length, full_kv.shape[2]), jnp.float32)

time: 169 us -> 148 us (0.88)
  blocking collectives: 81 us -> 64.4 us
  waiting for transfers between devices: 11.4 us -> 8.75 us
  matrix products: 13 us -> 10.8 us
    psum x1 -> x2, blocking collectives: 40.7 us -> 24.1 us  [the longest x1 12.1 us: on_device(): pair_sums = lax.psum(inner, 'prefix')]
    reduce_scatter x1, waiting for transfers between devices: 11.3 us -> 8.73 us  [on_device(): lax.psum_scatter(partial_value, 'prefix', scatter_dimension=1, tiled=True)]
    unnamed x58 -> x62, local copies, waits for them, and re-layouts: 9.16 us -> 9.81 us
where the time goes in v1:
time: 148 us; the launch traced here: 147 us
  blocking collectives  64.4 us (44%)
  between operations  28.8 us (19%)
  local copies, waits for them, and re-layouts  18.3 us (12%)
  other arithmetic  16.3 us (11%)
  matrix products  10.8 us (7%)
  waiting for transfers between devices  8.75 us (6%)
    psum x1, blocking collectives, on_device(): grad_prompt = lax.psum(owned, 'resp').astype(jnp.bfloat16)  24.7 us
    all_gather x1, blocking collectives, on_device(): full_kv = lax.all_gather(prompt_kv, 'prefix', axis=1, tiled=True)  15.6 us
    psum x1, blocking collectives, on_device(): pair_sums = lax.psum(inner, 'prefix')  12.1 us
    psum x1, blocking collectives, on_device(): inner = lax.psum(contrib, 'resp')  12 us
    unnamed x62, local copies, waits for them, and re-layouts  9.81 us
    reduce_scatter x1, waiting for transfers between devices, on_device(): lax.psum_scatter(partial_value, 'prefix', scatter_dimension=1, tiled=True)  8.73 us
  transfers between devices with their start and end apart: 1, of which 1 were waited for; matrix products, arithmetic and copies ran while one was open for 4% of the time, Pallas kernels for 0%

profile of v1, /device:TPU:0, one launch (start us, length us, event | category | flops | bytes accessed | tf_op | source)
XLA Modules:
  0.0 147.4 jit_solution(17230850235877271238)
XLA Ops:
  7.2 1.3 fusion.48
  18.3 1.9 %iota_compare_fusion.1 = (pred[2]{0:T(512)(128)(4,1)}, pred[2]{0:T(512)(128)(4,1)}) fusion(s32[]{:T(128)} %bitcast.23, s32[]{:T(128)} %bitcast.2), kind=kLoop, calls=%fused_computation.89 | loop fusion | flops 4 | bytes 12 | tf_op jit(solution)/shard_map/eq | solution.py:168
  21.5 0.6 copy-done.25
  22.8 1.2 compare_convert_fusion.1
  23.9 1.2 compare_convert_fusion
  25.2 15.6 %all_gather.3 = bf16[2,128,512]{2,1,0:T(8,128)(2,1)S(1)} all-gather(bf16[2,32,512]{2,1,0:T(8,128)(2,1)S(1)} %copy-done.21), channel_id=1, replica_groups=mesh['prefix'=4,'resp'=8] {'prefix'}, dimensions={1}, use_global_device_ids=true | all-gather | bytes 327680 | tf_op jit(solution)/shard_map/all_gather | solution.py:67
  43.4 0.6 fusion.44
  45.7 1.1 divide_convert_fusion.1
  48.2 0.8 copy-done.13
  49.1 1.4 slice_convert_fusion.1
  50.5 1.5 copy.68
  52.3 1.3 multiply_reduce_fusion.3
  53.5 1.2 fusion.36
  54.7 1.5 copy.79
  56.2 1.2 convolution_bitcast_fusion.2
  57.4 1.2 multiply_reduce_fusion.2
  58.7 1.2 fusion.37
  61.1 12.0 %psum.21 = f32[32]{0:T(128)S(1)} all-reduce(f32[32]{0:T(128)S(1)} %fusion.38), channel_id=1, replica_groups=mesh['prefix'=4,'resp'=8] {'resp'}, use_global_device_ids=true, to_apply=%region_12.13 | all-reduce | flops 32 | bytes 256 | tf_op jit(solution)/shard_map/psum | solution.py:92
  73.1 12.1 %psum.22 = f32[32]{0:T(128)S(1)} all-reduce(f32[32]{0:T(128)S(1)} %psum.21), channel_id=1, replica_groups=mesh['prefix'=4,'resp'=8] {'prefix'}, use_global_device_ids=true, to_apply=%region_13.14 | all-reduce | flops 32 | bytes 256 | tf_op jit(solution)/shard_map/psum | solution.py:93
  85.7 0.6 fusion.45
  88.2 1.4 multiply_reduce_fusion.1
  91.2 0.7 copy-done.27
  91.9 1.4 multiply_reduce_fusion
  95.6 0.9 select_add_fusion
  96.5 1.0 copy-done.3
  97.5 0.9 fusion.29
  98.8 0.6 copy-done.1
  104.2 0.7 copy-done.9
  105.4 0.7 maximum_maximum_fusion
  106.1 1.0 pad_maximum_fusion
  107.1 8.7 %reduce-scatter.2.cloned.1.call-done = f32[2,32,512]{2,1,0:T(8,128)} async-done(((f32[2,128,512]{2,1,0:T(8,128)}), f32[2,32,512]{2,1,0:T(8,128)}) %reduce-scatter.2.cloned.1.call-update) | async-done | bytes 131088 | tf_op jit(solution)/shard_map/reduce_scatter | solution.py:172
  115.9 24.7 %all-reduce.1 = bf16[2,32,512]{2,1,0:T(8,128)(2,1)} all-reduce(f32[2,32,512]{2,1,0:T(8,128)} %reduce-scatter.2.cloned.1.call-done), channel_id=1, replica_groups=mesh['prefix'=4,'resp'=8] {'resp'}, use_global_device_ids=true, to_apply=%region_17.18 | all-reduce | flops 32768 | bytes 196608 | tf_op jit(solution)/shard_map/psum | solution.py:173
  (109 shorter events, 16.1 us)
Async XLA Ops:
  7.2 108.7 %reduce-scatter.2.cloned.1.call-start = ((), (), s32[]{:S(2)}) async-start(), calls=%async_computation.1 | async-start | bytes 655360 | tf_op jit(solution)/shard_map/reduce_scatter | solution.py:172
  13.1 2.1 %copy-start.24 = (s32[32]{0:T(128)S(1)}, s32[32]{0:T(128)}, u32[]{:S(2)}) copy-start(s32[32]{0:T(128)} %param.14) | copy-start | bytes 388
  13.7 11.4 %copy-start.21 = (bf16[2,32,512]{2,1,0:T(8,128)(2,1)S(1)}, bf16[2,32,512]{2,1,0:T(8,128)(2,1)}, u32[]{:S(2)}) copy-start(bf16[2,32,512]{2,1,0:T(8,128)(2,1)} %param.8) | copy-start | bytes 196612
  21.5 0.7 copy-start.25
  42.2 1.0 copy-start.19
  42.4 4.7 %copy-start.15 = (bf16[128,256]{0,1:T(8,128)(2,1)}, bf16[128,256]{0,1:T(8,128)(2,1)S(1)}, u32[]{:S(2)}) copy-start(bf16[128,256]{0,1:T(8,128)(2,1)S(1)} %copy.59) | copy-start | bytes 196612
  42.4 1.6 %copy-start.12 = (bf16[2,128,1792]{2,1,0:T(8,128)(2,1)S(1)}, bf16[2,128,1792]{2,1,0:T(8,128)(2,1)}, u32[]{:S(2)}) copy-start(bf16[2,128,1792]{2,1,0:T(8,128)(2,1)} %param.9) | copy-start | bytes 2752516
  42.6 2.1 %copy-start.17 = (bf16[128,256]{0,1:T(8,128)(2,1)}, bf16[128,256]{0,1:T(8,128)(2,1)S(1)}, u32[]{:S(2)}) copy-start(bf16[128,256]{0,1:T(8,128)(2,1)S(1)} %copy.70) | copy-start | bytes 196612
  46.8 9.4 %copy-start = (bf16[2,7,128,128]{2,3,1,0:T(8,128)(2,1)}, bf16[2,7,128,128]{2,3,1,0:T(8,128)(2,1)S(1)}, u32[]{:S(2)}) copy-start(bf16[2,7,128,128]{2,3,1,0:T(8,128)(2,1)S(1)} %get-tuple-element.33) | copy-start | bytes 1376260
  47.9 1.2 copy-start.13
  49.1 2.9 %copy-start.2 = (bf16[2,7,128,128]{2,3,1,0:T(8,128)(2,1)}, bf16[2,7,128,128]{2,3,1,0:T(8,128)(2,1)S(1)}, u32[]{:S(2)}) copy-start(bf16[2,7,128,128]{2,3,1,0:T(8,128)(2,1)S(1)} %get-tuple-element.31) | copy-start | bytes 1376260
  49.1 3.2 %copy-start.6 = (bf16[2,7,128,128]{2,3,1,0:T(8,128)(2,1)}, bf16[2,7,128,128]{2,3,1,0:T(8,128)(2,1)S(1)}, u32[]{:S(2)}) copy-start(bf16[2,7,128,128]{2,3,1,0:T(8,128)(2,1)S(1)} %get-tuple-element.30) | copy-start | bytes 1376260
  56.2 1.2 copy-start.4
  73.1 12.1 %copy-start.26 = (f32[32]{0:T(128)S(1)}, f32[32]{0:T(128)}, u32[]{:S(2)}) copy-start(f32[32]{0:T(128)} %param.15) | copy-start | bytes 388
  87.6 0.6 copy-start.28
  88.2 1.4 copy-start.7
  90.3 0.8 copy-start.8
  91.2 0.7 copy-start.27
  91.9 1.4 copy-start.5
  94.0 0.8 copy-start.10
  94.9 0.7 copy-start.22
  94.9 0.7 copy-start.23
  96.5 1.0 copy-start.3
  98.5 1.0 copy-start.1
  99.5 0.8 copy-start.14
  101.0 0.8 copy-start.20
  101.9 1.0 copy-start.11
  102.5 0.9 copy-start.18
  103.9 1.0 copy-start.9
  103.9 1.0 copy-start.16
Sparse Core Ops, SparseCore 0:
  96.7 19.1 reduce-scatter.1
